TPU v7x, 32 devices: a whole 2x2x4 slice. The times are simulated.
32 devices in a mesh: dp: 8 (over y, x, core), tensor: 4 (over z).
Axes of the slice: x: 2, y: 2, z: 4, core: 2. Of those that a mesh axis runs over, the one named last changes fastest.
Arguments:
- attn_out: bfloat16 [3072, 4096], P('dp', 'tensor'), may hold values from -24 to 24
- out_grad: bfloat16 [3072, 4096], P('dp', 'tensor'), may hold values from -6 to 6
- proj_in: bfloat16 [64, 4096], P(None, 'tensor'), may hold values from -0.09375 to 0.09375
- proj_out: bfloat16 [64, 4096], P(None, 'tensor'), may hold values from -0.09375 to 0.09375
- targets: float32 [256, 64, 64], P(None, 'tensor'), may hold values from -6 to 6
Outputs:
- scores: float32 [48, 256], P('dp')
All inputs are finite; a program needn't handle non-finite values.
Results may differ from a plain program's by a relative error of at most 0.0015.
Values sent between devices are 32-bit elements; how exact they have to be, the bound alone decides.
A program may use at most 64 MiB of HBM per device.

v0:
```python
import jax
import jax.numpy as jnp
from jax import lax
from jax.sharding import PartitionSpec as P

LEN = 64
damping_ratio = 0.5
epsilon = 1e-06


def inner_rows(left, right):
    return lax.dot_general(
        left,
        right,
        (((1,), (1,)), ((), ())),
        precision=lax.Precision.HIGHEST,
        preferred_element_type=jnp.float32,
    )


def shards(attn_out, out_grad, proj_in, proj_out, targets):
    tok_rows = attn_out.shape[0]
    proj_rank = proj_in.shape[0]
    seq_count = tok_rows // LEN
    inputs_part = jnp.einsum("td,rd->tr", attn_out, proj_in, preferred_element_type=jnp.float32)
    grads_part = jnp.einsum("td,rd->tr", out_grad, proj_out, preferred_element_type=jnp.float32)
    inputs_low = lax.psum_scatter(inputs_part, "tensor", scatter_dimension=1, tiled=True)
    grads_low = lax.psum(grads_part, "tensor")
    part_width = inputs_low.shape[1]
    sample_grads = jnp.einsum(
        "sti,sto->sio",
        inputs_low.reshape(seq_count, LEN, part_width),
        grads_low.reshape(seq_count, LEN, proj_rank),
        precision=lax.Precision.HIGHEST,
    ).reshape(seq_count, part_width * proj_rank)
    target_rows = targets.reshape(targets.shape[0], part_width * proj_rank)
    gathered = lax.all_gather(sample_grads, "dp", axis=0, tiled=True)
    gram_matrix = inner_rows(gathered, gathered)
    cross_terms = inner_rows(gathered, target_rows)
    gram_matrix, cross_terms = lax.psum((gram_matrix, cross_terms), "tensor")
    trace_sum = jnp.trace(gram_matrix)
    samples = gram_matrix.shape[0]
    damping = damping_ratio * trace_sum / (samples * proj_rank * proj_rank) + epsilon
    system = gram_matrix / samples + damping * jnp.eye(samples, dtype=jnp.float32)
    factor = jnp.linalg.cholesky(system)
    solved = jax.scipy.linalg.cho_solve((factor, True), cross_terms)
    return lax.dynamic_slice_in_dim(solved, lax.axis_index("dp") * seq_count, seq_count, 0)


def solution(mesh):
    in_specs = (
        P("dp", "tensor"),
        P("dp", "tensor"),
        P(None, "tensor"),
        P(None, "tensor"),
        P(None, "tensor", None),
    )
    out_specs = P("dp", None)
    return jax.shard_map(shards, mesh=mesh, in_specs=in_specs, out_specs=out_specs, check_vma=False)
```

profile of v0, /device:TPU:0, one launch (start us, length us, event | category | flops | bytes accessed | tf_op | source)
XLA Modules:
  0.0 116.2 jit_solution(16831811706130720864)
XLA Ops:
  6.5 0.0 copy-start
  6.5 0.0 copy-start.1
  6.5 0.0 reduce-scatter.2.cloned.1.call-start
  6.5 0.0 copy-start.2
  6.5 2.3 %fusion.8 = f32[384,64]{0,1:T(8,128)} fusion(bf16[384,1024]{1,0:T(8,128)(2,1)} %param.5, bf16[64,1024]{1,0:T(8,128)(2,1)} %param.7), kind=kOutput, calls=%fused_computation.17 | convolution fusion | flops 50331648 | bytes 1015808 | tf_op jit(solution)/shard_map/td,rd->tr/dot_general | solution.py:25
  8.8 0.0 reduce-scatter.2.cloned.1.call-update
  8.8 0.0 all-reduce.3.cloned.1.call-start
  8.9 0.0 copy-done.1
  8.9 0.0 copy-done.2
  8.9 1.0 fusion.9
  9.9 0.0 all-reduce.3.cloned.1.call-update
  10.0 21.8 %reduce-scatter.2.cloned.1.call-done = f32[384,16]{0,1:T(8,128)} async-done(((f32[384,64]{0,1:T(8,128)}), f32[384,16]{0,1:T(8,128)}) %reduce-scatter.2.cloned.1.call-update) | async-done | bytes 24592 | tf_op jit(solution)/shard_map/reduce_scatter | solution.py:27
  31.7 0.8 reshape.25
  32.6 34.7 %all-reduce.3.cloned.1.call-done = f32[6,64,64]{2,1,0:T(8,128)} async-done(((f32[6,64,64]{2,1,0:T(8,128)}), f32[6,64,64]{2,1,0:T(8,128)}) %all-reduce.3.cloned.1.call-update) | async-done | bytes 98320 | tf_op jit(solution)/shard_map/psum | solution.py:28
  67.2 1.2 %fusion = f32[6,16,64]{2,1,0:T(8,128)S(1)} fusion(f32[6,64,64]{2,1,0:T(8,128)} %all-reduce.3.cloned.1.call-done, f32[6,64,16]{1,0,2:T(8,128)S(1)} %reshape.25), kind=kOutput, calls=%fused_computation | convolution fusion | flops 4718592 | bytes 147456 | tf_op jit(solution)/shard_map/sti,sto->sio/dot_general | solution.py:30
  68.5 0.1 reshape.29
  68.5 9.2 %all-gather = f32[8,6,1024]{2,1,0:T(8,128)S(1)} all-gather(f32[1,6,1024]{2,1,0:T(8,128)S(1)} %reshape.29), channel_id=1, replica_groups=mesh['dp'=8,'tensor'=4] {'dp'}, dimensions={0}, use_global_device_ids=true | all-gather | bytes 221184 | tf_op jit(solution)/shard_map/all_gather | solution.py:37
  77.7 0.3 fusion.10
  78.1 0.0 copy-done
  78.1 0.6 fusion.11
  78.7 18.8 %all-reduce = (f32[48,256]{1,0:T(8,128)S(1)}, f32[48,48]{1,0:T(8,128)S(1)}) all-reduce(f32[48,256]{1,0:T(8,128)S(1)} %fusion.11, f32[48,48]{1,0:T(8,128)S(1)} %fusion.10), channel_id=1, replica_groups=mesh['dp'=8,'tensor'=4] {'tensor'}, use_global_device_ids=true, to_apply=%region_6.7 | all-reduce | flops 14592 | bytes 116736 | tf_op jit(solution)/shard_map/psum | solution.py:40
  97.5 0.6 select_reduce_fusion.1
  98.8 0.1 copy.14
  98.9 4.4 %cholesky.17 = f32[48,48]{1,0:T(8,128)S(1)} custom-call(f32[48,48]{1,0:T(8,128)S(1)} %fusion.7), custom_call_target="Cholesky" | custom-call | tf_op jit(solution)/shard_map/jit(cholesky)/cholesky | solution.py:45
  103.3 0.6 compare_reduce_fusion
  103.9 0.7 fusion.2
  104.6 3.7 %custom-call.10 = f32[1,48,48]{1,2,0:T(8,128)S(1)} custom-call(f32[1,48,48]{2,1,0:T(8,128)S(1)} %fusion.2), custom_call_target="InvertDiagBlocksLowerTriangular" | custom-call | tf_op jit(solution)/shard_map/jit(_cho_solve)/triangular_solve | solution.py:46
  108.3 0.2 fusion.5
  108.5 0.2 fusion.3
  108.7 0.6 constant_dynamic-slice_fusion
  (4 shorter events, 0.1 us)
Async XLA Ops:
  6.5 71.5 %copy-start = (f32[256,16,64]{0,2,1:T(8,128)S(1)}, f32[256,16,64]{0,2,1:T(8,128)}, u32[]{:S(2)}) copy-start(f32[256,16,64]{0,2,1:T(8,128)} %param.9) | copy-start | bytes 3145732
  6.5 2.4 %copy-start.1 = (bf16[384,1024]{1,0:T(8,128)(2,1)S(1)}, bf16[384,1024]{1,0:T(8,128)(2,1)}, u32[]{:S(2)}) copy-start(bf16[384,1024]{1,0:T(8,128)(2,1)} %param.6) | copy-start | bytes 2359300
  6.5 25.2 %reduce-scatter.2.cloned.1.call-start = ((), (), s32[]{:S(2)}) async-start(), calls=%async_computation.1 | async-start | bytes 122880 | tf_op jit(solution)/shard_map/reduce_scatter | solution.py:27
  6.5 2.4 %copy-start.2 = (bf16[64,1024]{1,0:T(8,128)(2,1)S(1)}, bf16[64,1024]{1,0:T(8,128)(2,1)}, u32[]{:S(2)}) copy-start(bf16[64,1024]{1,0:T(8,128)(2,1)} %param.8) | copy-start | bytes 393220
  8.8 58.4 %all-reduce.3.cloned.1.call-start = ((), (), s32[]{:S(2)}) async-start(), calls=%async_computation.2 | async-start | bytes 393216 | tf_op jit(solution)/shard_map/psum | solution.py:28
Sparse Core Ops, SparseCore 0:
  9.6 22.1 reduce-scatter.1
  34.1 33.1 all-reduce.2
where the time goes:
time: 116 us
  waiting for transfers between devices  56.5 us (49%)
  blocking collectives  28 us (24%)
  between operations  14.2 us (12%)
  other arithmetic  10 us (9%)
  matrix products  5.86 us (5%)
  local copies, waits for them, and re-layouts  1.62 us (1%)
    psum x1, waiting for transfers between devices, shards(): grads_low = lax.psum(grads_part, 'tensor')  34.7 us
    reduce_scatter x1, waiting for transfers between devices, shards(): lax.psum_scatter(inputs_part, 'tensor', scatter_dimension=1, tiled=True)  21.8 us
    psum x1, blocking collectives, shards(): gram_matrix, cross_terms = lax.psum((gram_matrix, cross_terms), 'tensor')  18.8 us
    all_gather x1, blocking collectives, shards(): gathered = lax.all_gather(sample_grads, 'dp', axis=0, tiled=True)  9.17 us
    another operation x3, other arithmetic, shards(): factor = jnp.linalg.cholesky(system)  5.05 us
    another operation x2, other arithmetic, shards(): solved = jax.scipy.linalg.cho_solve((factor, True), cross_terms)  4.32 us
  transfers between devices with their start and end apart: 2, of which 2 were waited for; matrix products, arithmetic and copies ran while one was open for 2% of the time, Pallas kernels for 0%

commit v1 on v0

--- a/solution.py
+++ b/solution.py
@@ -25,7 +25,7 @@
     inputs_part = jnp.einsum("td,rd->tr", attn_out, proj_in, preferred_element_type=jnp.float32)
     grads_part = jnp.einsum("td,rd->tr", out_grad, proj_out, preferred_element_type=jnp.float32)
     inputs_low = lax.psum_scatter(inputs_part, "tensor", scatter_dimension=1, tiled=True)
-    grads_low = lax.psum(grads_part, "tensor")
+    grads_low = jnp.sum(lax.all_gather(grads_part, "tensor"), axis=0)
     part_width = inputs_low.shape[1]
     sample_grads = jnp.einsum(
         "sti,sto->sio",

time: 116 us -> 79.5 us (0.69)
  waiting for transfers between devices: 56.5 us -> 5.22 us
  blocking collectives: 28 us -> 43.5 us
  matrix products: 5.86 us -> 4.24 us
    psum x1 -> x0, waiting for transfers between devices: 34.7 us -> none  [shards(): grads_low = lax.psum(grads_part, 'tensor')]
    all_gather x0 -> x1, blocking collectives: none -> 16.9 us  [shards(): grads_low = jnp.sum(lax.all_gather(grads_part, 'tensor'), axis=0)]
    reduce_scatter x1, waiting for transfers between devices: 21.8 us -> 5.2 us  [shards(): lax.psum_scatter(inputs_part, 'tensor', scatter_dimension=1, tiled=True)]
    psum x1, blocking collectives: 18.8 us -> 17.4 us  [shards(): gram_matrix, cross_terms = lax.psum((gram_matrix, cross_terms), 'tensor')]
  transfers between devices with their start and end apart: 2 -> 1, of which waited for: 2 -> 1; matrix products, arithmetic and copies ran while one was open for 2% -> 1% of each run, Pallas kernels for 0% -> 0%
where the time goes in v1:
time: 79.5 us; the launch traced here: 79.2 us
  blocking collectives  43.5 us (55%)
  between operations  14.2 us (18%)
  other arithmetic  10.2 us (13%)
  waiting for transfers between devices  5.22 us (7%)
  matrix products  4.24 us (5%)
  local copies, waits for them, and re-layouts  1.88 us (2%)
    psum x1, blocking collectives, shards(): gram_matrix, cross_terms = lax.psum((gram_matrix, cross_terms), 'tensor')  17.4 us
    all_gather x1, blocking collectives, shards(): grads_low = jnp.sum(lax.all_gather(grads_part, 'tensor'), axis=0)  16.9 us
    all_gather x1, blocking collectives, shards(): gathered = lax.all_gather(sample_grads, 'dp', axis=0, tiled=True)  9.2 us
    reduce_scatter x1, waiting for transfers between devices, shards(): lax.psum_scatter(inputs_part, 'tensor', scatter_dimension=1, tiled=True)  5.2 us
    another operation x3, other arithmetic, shards(): factor = jnp.linalg.cholesky(system)  5.05 us
    another operation x2, other arithmetic, shards(): solved = jax.scipy.linalg.cho_solve((factor, True), cross_terms)  4.32 us
    dot_general x1, matrix products, shards(): jnp.einsum('td,rd->tr', attn_out, proj_in, preferred_element_type=jnp.flo...  2.26 us
  transfers between devices with their start and end apart: 1, of which 1 were waited for; matrix products, arithmetic and copies ran while one was open for 1% of the time, Pallas kernels for 0%

profile of v1, /device:TPU:0, one launch (start us, length us, event | category | flops | bytes accessed | tf_op | source)
XLA Modules:
  0.0 79.2 jit_solution(11738905890525213787)
XLA Ops:
  6.5 0.0 copy-start
  6.5 0.0 copy-start.1
  6.5 0.0 reduce-scatter.2.cloned.1.call-start
  6.5 0.0 copy-start.2
  6.5 2.3 %fusion.8 = f32[384,64]{0,1:T(8,128)} fusion(bf16[384,1024]{1,0:T(8,128)(2,1)} %param.5, bf16[64,1024]{1,0:T(8,128)(2,1)} %param.7), kind=kOutput, calls=%fused_computation.17 | convolution fusion | flops 50331648 | bytes 1015808 | tf_op jit(solution)/shard_map/td,rd->tr/dot_general | solution.py:25
  8.8 0.0 reduce-scatter.2.cloned.1.call-update
  8.8 0.0 copy-done.1
  8.8 0.0 copy-done.2
  8.9 0.4 fusion.9
  9.2 16.9 %all-gather = f32[1536,64]{0,1:T(8,128)S(1)} all-gather(f32[384,64]{0,1:T(8,128)S(1)} %fusion.9), channel_id=2, replica_groups=mesh['dp'=8,'tensor'=4] {'tensor'}, dimensions={0}, use_global_device_ids=true | all-gather | bytes 491520 | tf_op jit(solution)/shard_map/all_gather | solution.py:28
  26.1 0.1 reshape.29
  26.2 0.2 reduce_sum.19
  26.5 0.1 copy.16
  26.6 5.2 %reduce-scatter.2.cloned.1.call-done = f32[384,16]{0,1:T(8,128)} async-done(((f32[384,64]{0,1:T(8,128)}), f32[384,16]{0,1:T(8,128)}) %reduce-scatter.2.cloned.1.call-update) | async-done | bytes 24592 | tf_op jit(solution)/shard_map/reduce_scatter | solution.py:27
  31.8 0.8 %reshape.25 = f32[6,64,16]{1,0,2:T(8,128)S(1)} reshape(f32[384,16]{0,1:T(8,128)} %reduce-scatter.2.cloned.1.call-done) | data formatting | bytes 49152 | tf_op jit(solution)/shard_map/reshape | solution.py:32
  32.6 0.3 fusion
  32.9 0.1 reshape.30
  33.0 9.2 %all-gather.1 = f32[8,6,1024]{2,1,0:T(8,128)S(1)} all-gather(f32[1,6,1024]{2,1,0:T(8,128)S(1)} %reshape.30), channel_id=1, replica_groups=mesh['dp'=8,'tensor'=4] {'dp'}, dimensions={0}, use_global_device_ids=true | all-gather | bytes 221184 | tf_op jit(solution)/shard_map/all_gather | solution.py:37
  42.2 0.3 fusion.10
  42.5 0.0 copy-done
  42.5 0.6 fusion.11
  43.2 17.4 %all-reduce = (f32[48,256]{1,0:T(8,128)S(1)}, f32[48,48]{1,0:T(8,128)S(1)}) all-reduce(f32[48,256]{1,0:T(8,128)S(1)} %fusion.11, f32[48,48]{1,0:T(8,128)S(1)} %fusion.10), channel_id=1, replica_groups=mesh['dp'=8,'tensor'=4] {'tensor'}, use_global_device_ids=true, to_apply=%region_6.7 | all-reduce | flops 14592 | bytes 116736 | tf_op jit(solution)/shard_map/psum | solution.py:40
  60.6 0.6 select_reduce_fusion.1
  61.8 0.1 copy.15
  61.9 4.4 %cholesky.17 = f32[48,48]{1,0:T(8,128)S(1)} custom-call(f32[48,48]{1,0:T(8,128)S(1)} %fusion.7), custom_call_target="Cholesky" | custom-call | tf_op jit(solution)/shard_map/jit(cholesky)/cholesky | solution.py:45
  66.4 0.6 compare_reduce_fusion
  67.0 0.7 fusion.2
  67.7 3.7 %custom-call.10 = f32[1,48,48]{1,2,0:T(8,128)S(1)} custom-call(f32[1,48,48]{2,1,0:T(8,128)S(1)} %fusion.2), custom_call_target="InvertDiagBlocksLowerTriangular" | custom-call | tf_op jit(solution)/shard_map/jit(_cho_solve)/triangular_solve | solution.py:46
  71.3 0.2 fusion.5
  71.6 0.2 fusion.3
  71.8 0.6 constant_dynamic-slice_fusion
  (4 shorter events, 0.1 us)
Async XLA Ops:
  6.5 36.0 %copy-start = (f32[256,16,64]{0,2,1:T(8,128)S(1)}, f32[256,16,64]{0,2,1:T(8,128)}, u32[]{:S(2)}) copy-start(f32[256,16,64]{0,2,1:T(8,128)} %param.9) | copy-start | bytes 3145732
  6.5 2.3 %copy-start.1 = (bf16[384,1024]{1,0:T(8,128)(2,1)S(1)}, bf16[384,1024]{1,0:T(8,128)(2,1)}, u32[]{:S(2)}) copy-start(bf16[384,1024]{1,0:T(8,128)(2,1)} %param.6) | copy-start | bytes 2359300
  6.5 25.3 %reduce-scatter.2.cloned.1.call-start = ((), (), s32[]{:S(2)}) async-start(), calls=%async_computation.1 | async-start | bytes 122880 | tf_op jit(solution)/shard_map/reduce_scatter | solution.py:27
  6.5 2.3 %copy-start.2 = (bf16[64,1024]{1,0:T(8,128)(2,1)S(1)}, bf16[64,1024]{1,0:T(8,128)(2,1)}, u32[]{:S(2)}) copy-start(bf16[64,1024]{1,0:T(8,128)(2,1)} %param.8) | copy-start | bytes 393220
Sparse Core Ops, SparseCore 0:
  9.6 22.1 reduce-scatter.1
